TPU v7x, 32 devices: a whole 2x2x4 slice. The times are simulated.
32 devices in a mesh: section: 2 (over x), dp: 4 (over z), mp: 4 (over y, core).
Axes of the slice: x: 2, y: 2, z: 4, core: 2. Of those that a mesh axis runs over, the one named last changes fastest.
Arguments:
- text_feats: bfloat16 [4096, 512], P('dp'), may hold values from -48 to 48
- image_feats: bfloat16 [4096, 512], P(('dp', 'mp')), may hold values from -48 to 48
- logit_scale: float32 [1], replicated, may hold values from 10 to 320
- layer_inputs: bfloat16 [2, 4096, 512], P('section', 'dp'), may hold values from -6 to 6
- w_in: bfloat16 [2, 512, 2048], P('section', None, 'mp'), may hold values from -0.25 to 0.25
- w_out: bfloat16 [2, 2048, 512], P('section', 'mp'), may hold values from -0.125 to 0.125
Outputs:
- image_grad: bfloat16 [4096, 512], P(('dp', 'mp'))
- input_grad: bfloat16 [4096, 512], P('dp', 'section')
- w_in_grad: float32 [2, 512, 2048], P('section', 'dp', 'mp')
- w_out_grad_t: float32 [2, 512, 2048], P('section', 'dp', 'mp')
All inputs are finite; a program needn't handle non-finite values.
Results may differ from a plain program's by a relative error of at most 0.017.
Values may be sent and summed in bfloat16 or wider, within the bound.
A program may use at most 128 MiB of HBM per device.

v0:
```python
import jax
import jax.numpy as jnp
from jax import lax
from jax.sharding import PartitionSpec as P

MICRO = 4


def shifted(block, axis, distance):
    devices = range(lax.axis_size(axis))
    route = [(i - distance, i) for i in devices if i - distance in devices]
    return lax.ppermute(block, axis, route)


def spread(value, axis, source):
    kept = jnp.where(lax.axis_index(axis) == source, value, 0).astype(value.dtype)
    return lax.psum(kept, axis)


def unit_rows(values):
    wide = values.astype(jnp.float32)
    length = jnp.sqrt(jnp.sum(wide * wide, axis=1, keepdims=True) + 1.0)
    return (wide / length, length)


def unit_backward(unit, length, grad_unit):
    return (grad_unit - unit * jnp.sum(unit * grad_unit, axis=1, keepdims=True)) / length


def quick_gelu(values):
    return values * jax.nn.sigmoid(1.702 * values)


def quick_slope(values):
    sigm = jax.nn.sigmoid(1.702 * values)
    return sigm + 1.702 * values * sigm * (1.0 - sigm)


def contract_rows(left_side, right_side):
    return lax.dot_general(
        left_side, right_side, (((0,), (0,)), ((), ())), preferred_element_type=jnp.float32
    )


def contract_cols(left_side, right_side):
    return lax.dot_general(
        left_side, right_side, (((1,), (1,)), ((), ())), preferred_element_type=jnp.float32
    )


def body(text_feats, image_feats, logit_scale, layer_inputs, w_in, w_out):
    logit_mult = logit_scale[0]
    mp_count = lax.axis_size("mp")
    segment_count = lax.axis_size("section")
    dp_index = lax.axis_index("dp")
    mp_index = lax.axis_index("mp")
    segment_index = lax.axis_index("section")
    row_count = text_feats.shape[0]
    own_rows = image_feats.shape[0]
    text_unit, text_length = unit_rows(text_feats)
    image_unit, image_length = unit_rows(image_feats)
    text_low = text_unit.astype(jnp.bfloat16)
    image_low = image_unit.astype(jnp.bfloat16)
    columns = lax.all_gather(image_low, "dp", axis=0, tiled=True)
    column_total_count = columns.shape[0]
    scores = logit_mult * contract_cols(text_low, columns)
    text_ids = dp_index * row_count + jnp.arange(row_count, dtype=jnp.int32)
    column_pos = jnp.arange(column_total_count, dtype=jnp.int32)
    image_ids = (column_pos // own_rows * mp_count + mp_index) * own_rows + column_pos % own_rows
    positive = (text_ids[:, None] == image_ids[None, :]).astype(jnp.float32)
    row_peak = lax.pmax(jnp.max(scores, axis=1), "mp")
    column_peak = lax.pmax(jnp.max(scores, axis=0), "dp")
    row_total = lax.psum(jnp.sum(jnp.exp(scores - row_peak[:, None]), axis=1), "mp")
    column_local = jnp.sum(jnp.exp(scores - column_peak[None, :]), axis=0)
    column_total = lax.psum(column_local, "dp")
    row_prob = jnp.exp(scores - row_peak[:, None]) / row_total[:, None]
    column_prob = jnp.exp(scores - column_peak[None, :]) / column_total[None, :]
    score_grad = (0.5 * (row_prob + column_prob) - positive).astype(jnp.bfloat16)
    text_share = logit_mult * jnp.dot(score_grad, columns, preferred_element_type=jnp.float32)
    text_unit_grad = lax.psum(text_share, "mp")
    top_grad = unit_backward(text_unit, text_length, text_unit_grad).astype(jnp.bfloat16)
    image_unit_grad = lax.psum_scatter(
        (logit_mult * contract_rows(score_grad, text_low)).astype(jnp.bfloat16),
        "dp",
        scatter_dimension=0,
        tiled=True,
    ).astype(jnp.float32)
    image_grad = unit_backward(image_unit, image_length, image_unit_grad).astype(jnp.bfloat16)
    segment_inputs = layer_inputs[0]
    w_first = w_in[0]
    w_second = w_out[0]
    step_rows = row_count // MICRO
    last_segment = segment_count - 1
    time_steps = MICRO + segment_count - 1
    is_last = segment_index == last_segment
    is_first = segment_index == 0
    incoming = jnp.zeros((step_rows, segment_inputs.shape[1]), jnp.bfloat16)
    grad_first = jnp.zeros(w_first.shape, jnp.float32)
    grad_second = jnp.zeros(w_first.shape, jnp.float32)
    finished = jnp.zeros((row_count, segment_inputs.shape[1]), jnp.bfloat16)
    for time_step in range(time_steps):
        micro_slot = time_step - last_segment + segment_index
        active = jnp.logical_and(micro_slot >= 0, micro_slot < MICRO)
        row_start = jnp.clip(micro_slot, 0, MICRO - 1) * step_rows
        top_start = min(time_step, MICRO - 1) * step_rows
        top_piece = top_grad[top_start : top_start + step_rows]
        grad_now = jnp.where(is_last, top_piece, incoming)
        inputs_now = lax.dynamic_slice_in_dim(segment_inputs, row_start, step_rows, 0)
        pre_act = jnp.dot(inputs_now, w_first, preferred_element_type=jnp.float32)
        activation = quick_gelu(pre_act).astype(jnp.bfloat16)
        back_grad = contract_cols(grad_now, w_second)
        pre_grad = (back_grad * quick_slope(pre_act)).astype(jnp.bfloat16)
        unit_share = contract_cols(pre_grad, w_first)
        summed = lax.psum(unit_share.astype(jnp.bfloat16), "mp").astype(jnp.float32)
        grad_prev = (grad_now.astype(jnp.float32) + summed).astype(jnp.bfloat16)
        weight = active.astype(jnp.float32)
        grad_first = grad_first + weight * contract_rows(inputs_now, pre_grad)
        grad_second = grad_second + weight * contract_rows(grad_now, activation)
        updated = lax.dynamic_update_slice_in_dim(finished, grad_prev, row_start, 0)
        finished = jnp.where(jnp.logical_and(active, is_first), updated, finished)
        if time_step + 1 < time_steps:
            incoming = shifted(grad_prev, "section", -1)
    whole_grad = spread(finished, "section", 0)
    feature_width = whole_grad.shape[1] // segment_count
    feature_start = segment_index * feature_width
    input_grad = lax.dynamic_slice_in_dim(whole_grad, feature_start, feature_width, 1)
    first_sum, second_sum = (
        lax.psum_scatter(
            grad_first.astype(jnp.bfloat16), "dp", scatter_dimension=0, tiled=True
        ).astype(jnp.float32),
        lax.psum_scatter(
            grad_second.astype(jnp.bfloat16), "dp", scatter_dimension=0, tiled=True
        ).astype(jnp.float32),
    )
    return (image_grad, input_grad, first_sum[None], second_sum[None])


def solution(mesh):
    placed = (
        P("dp", None),
        P(("dp", "mp"), None),
        P(),
        P("section", "dp", None),
        P("section", None, "mp"),
        P("section", "mp", None),
    )
    return jax.shard_map(
        body,
        mesh=mesh,
        in_specs=placed,
        out_specs=(
            P(("dp", "mp"), None),
            P("dp", "section"),
            P("section", "dp", "mp"),
            P("section", "dp", "mp"),
        ),
        check_vma=False,
    )
```

profile of v0, /device:TPU:0, one launch (start us, length us, event | category | flops | bytes accessed | tf_op | source)
XLA Modules:
  0.0 491.8 jit_solution(6473197469235849443)
XLA Ops:
  12.5 28.6 %all-gather.2.cloned.1.call-done = bf16[1024,512]{1,0:T(8,128)(2,1)} async-done(((bf16[256,512]{1,0:T(8,128)(2,1)}), bf16[1024,512]{1,0:T(8,128)(2,1)}) %all-gather.2.cloned.1.call-update) | async-done | bytes 1048592 | tf_op jit(solution)/shard_map/all_gather | solution.py:64
  41.1 4.5 multiply_reduce_fusion.1
  45.7 6.0 %pmax.14 = f32[1024]{0:T(1024)S(1)} all-reduce(f32[1024]{0:T(1024)S(1)} %get-tuple-element.14), channel_id=1, replica_groups=mesh['section'=2,'dp'=4,'mp'=4] {'mp'}, use_global_device_ids=true, to_apply=%region_3.4 | all-reduce | flops 1024 | bytes 8192 | tf_op jit(solution)/shard_map/pmax | solution.py:71
  51.7 3.2 fusion
  54.9 10.9 %pmax.15 = f32[1024]{0:T(1024)S(1)} all-reduce(f32[1024]{0:T(1024)S(1)} %get-tuple-element.5), channel_id=1, replica_groups=mesh['section'=2,'dp'=4,'mp'=4] {'dp'}, use_global_device_ids=true, to_apply=%region_7.8 | all-reduce | flops 1024 | bytes 8192 | tf_op jit(solution)/shard_map/pmax | solution.py:72
  65.8 2.9 fusion.1
  68.7 8.4 %psum.64 = f32[1024]{0:T(1024)S(1)} all-reduce(f32[1024]{0:T(1024)S(1)} %fusion.1), channel_id=1, replica_groups=mesh['section'=2,'dp'=4,'mp'=4] {'dp'}, use_global_device_ids=true, to_apply=%region_9.10 | all-reduce | flops 1024 | bytes 8192 | tf_op jit(solution)/shard_map/psum | solution.py:75
  77.1 5.7 %psum.63 = f32[1024]{0:T(1024)S(1)} all-reduce(f32[1024]{0:T(1024)S(1)} %get-tuple-element.4), channel_id=1, replica_groups=mesh['section'=2,'dp'=4,'mp'=4] {'mp'}, use_global_device_ids=true, to_apply=%region_5.6 | all-reduce | flops 1024 | bytes 8192 | tf_op jit(solution)/shard_map/psum | solution.py:73
  82.8 3.9 subtract_convert_fusion
  92.0 49.2 %all-reduce.8.cloned.1.call-done = f32[1024,512]{1,0:T(8,128)} async-done(((f32[1024,512]{1,0:T(8,128)}), f32[1024,512]{1,0:T(8,128)}) %all-reduce.8.cloned.1.call-update) | async-done | bytes 2097168 | tf_op jit(solution)/shard_map/psum | solution.py:80
  147.1 32.5 %all-reduce.10.cloned.1.call-done = bf16[256,512]{1,0:T(8,128)(2,1)} async-done(((bf16[256,512]{1,0:T(8,128)(2,1)}), bf16[256,512]{1,0:T(8,128)(2,1)}) %all-reduce.10.cloned.1.call-update) | async-done | bytes 262160 | tf_op jit(solution)/shard_map/psum | solution.py:114
  184.0 6.8 %collective-permute-done = bf16[256,512]{1,0:T(8,128)(2,1)S(1)} collective-permute-done((bf16[256,512]{1,0:T(8,128)(2,1)S(1)}, bf16[256,512]{1,0:T(8,128)(2,1)S(1)}, u32[]{:S(2)}, u32[]{:S(2)}) %collective-permute-start) | collective-permute-done | bytes 262176 | tf_op jit(solution)/shard_map/ppermute | solution.py:12
  194.1 32.4 %all-reduce.12.cloned.1.call-done = bf16[256,512]{1,0:T(8,128)(2,1)} async-done(((bf16[256,512]{1,0:T(8,128)(2,1)}), bf16[256,512]{1,0:T(8,128)(2,1)}) %all-reduce.12.cloned.1.call-update) | async-done | bytes 262160 | tf_op jit(solution)/shard_map/psum | solution.py:114
  229.9 6.9 %collective-permute-done.1 = bf16[256,512]{1,0:T(8,128)(2,1)} collective-permute-done((bf16[256,512]{1,0:T(8,128)(2,1)S(1)}, bf16[256,512]{1,0:T(8,128)(2,1)}, u32[]{:S(2)}, u32[]{:S(2)}) %collective-permute-start.1) | collective-permute-done | bytes 262176 | tf_op jit(solution)/shard_map/ppermute | solution.py:12
  241.1 32.4 %all-reduce.14.cloned.1.call-done = bf16[256,512]{1,0:T(8,128)(2,1)} async-done(((bf16[256,512]{1,0:T(8,128)(2,1)}), bf16[256,512]{1,0:T(8,128)(2,1)}) %all-reduce.14.cloned.1.call-update) | async-done | bytes 262160 | tf_op jit(solution)/shard_map/psum | solution.py:114
  277.0 7.1 %collective-permute-done.2 = bf16[256,512]{1,0:T(8,128)(2,1)} collective-permute-done((bf16[256,512]{1,0:T(8,128)(2,1)}, bf16[256,512]{1,0:T(8,128)(2,1)}, u32[]{:S(2)}, u32[]{:S(2)}) %collective-permute-start.2) | collective-permute-done | bytes 262176 | tf_op jit(solution)/shard_map/ppermute | solution.py:12
  288.1 32.4 %all-reduce.16.cloned.1.call-done = bf16[256,512]{1,0:T(8,128)(2,1)} async-done(((bf16[256,512]{1,0:T(8,128)(2,1)}), bf16[256,512]{1,0:T(8,128)(2,1)}) %all-reduce.16.cloned.1.call-update) | async-done | bytes 262160 | tf_op jit(solution)/shard_map/psum | solution.py:114
  324.3 6.9 %collective-permute-done.3 = bf16[256,512]{1,0:T(8,128)(2,1)} collective-permute-done((bf16[256,512]{1,0:T(8,128)(2,1)}, bf16[256,512]{1,0:T(8,128)(2,1)}, u32[]{:S(2)}, u32[]{:S(2)}) %collective-permute-start.3) | collective-permute-done | bytes 262176 | tf_op jit(solution)/shard_map/ppermute | solution.py:12
  335.2 4.0 multiply_convert_fusion
  350.5 17.1 %all-reduce.18.cloned.1.call-done = bf16[256,512]{1,0:T(8,128)(2,1)} async-done(((bf16[256,512]{1,0:T(8,128)(2,1)}), bf16[256,512]{1,0:T(8,128)(2,1)}) %all-reduce.18.cloned.1.call-update) | async-done | bytes 262160 | tf_op jit(solution)/shard_map/psum | solution.py:114
  371.8 25.4 %reduce-scatter.4.cloned.1.call-done = bf16[256,512]{1,0:T(8,128)(2,1)} async-done(((bf16[1024,512]{1,0:T(8,128)(2,1)}), bf16[256,512]{1,0:T(8,128)(2,1)}) %reduce-scatter.4.cloned.1.call-update) | async-done | bytes 262160 | tf_op jit(solution)/shard_map/reduce_scatter | solution.py:82
  400.2 20.2 %reduce-scatter.6.cloned.1.call-done = bf16[128,512]{1,0:T(8,128)(2,1)} async-done(((bf16[512,512]{1,0:T(8,128)(2,1)}), bf16[128,512]{1,0:T(8,128)(2,1)}) %reduce-scatter.6.cloned.1.call-update) | async-done | bytes 131088 | tf_op jit(solution)/shard_map/reduce_scatter | solution.py:128
  422.1 20.6 %reduce-scatter.8.cloned.1.call-done = bf16[128,512]{1,0:T(8,128)(2,1)} async-done(((bf16[512,512]{1,0:T(8,128)(2,1)}), bf16[128,512]{1,0:T(8,128)(2,1)}) %reduce-scatter.8.cloned.1.call-update) | async-done | bytes 131088 | tf_op jit(solution)/shard_map/reduce_scatter | solution.py:131
  444.3 39.1 %all-reduce.20.cloned.1.call-done = bf16[1024,512]{1,0:T(8,128)(2,1)} async-done(((bf16[1024,512]{1,0:T(8,128)(2,1)}), bf16[1024,512]{1,0:T(8,128)(2,1)}) %all-reduce.20.cloned.1.call-update) | async-done | bytes 1048592 | tf_op jit(solution)/shard_map/psum | solution.py:17
  (142 shorter events, 69.7 us)
Async XLA Ops:
  7.2 83.5 %copy-start = (bf16[1,1024,512]{2,1,0:T(8,128)(2,1)S(1)}, bf16[1,1024,512]{2,1,0:T(8,128)(2,1)}, u32[]{:S(2)}) copy-start(bf16[1,1024,512]{2,1,0:T(8,128)(2,1)} %param.9) | copy-start | bytes 3145732
  7.2 34.0 %copy-start.2 = (bf16[1024,512]{1,0:T(8,128)(2,1)S(1)}, bf16[1024,512]{1,0:T(8,128)(2,1)}, u32[]{:S(2)}) copy-start(bf16[1024,512]{1,0:T(8,128)(2,1)} %param.6) | copy-start | bytes 3145732
  7.2 33.9 %all-gather.2.cloned.1.call-start = ((), (), s32[]{:S(2)}) async-start(), calls=%async_computation.3 | async-start | bytes 1310720 | tf_op jit(solution)/shard_map/all_gather | solution.py:64
  10.3 130.9 %all-reduce.8.cloned.1.call-start = ((), (), s32[]{:S(2)}) async-start(), calls=%async_computation.5 | async-start | bytes 4194304 | tf_op jit(solution)/shard_map/psum | solution.py:80
  90.6 88.9 %all-reduce.10.cloned.1.call-start = ((), (), s32[]{:S(2)}) async-start(), calls=%async_computation.6 | async-start | bytes 524288 | tf_op jit(solution)/shard_map/psum | solution.py:114
  92.0 51.9 %copy-start.23 = (f32[256,512]{1,0:T(8,128)}, f32[256,512]{1,0:T(8,128)S(1)}, u32[]{:S(2)}) copy-start(f32[256,512]{1,0:T(8,128)S(1)} %fusion.35) | copy-start | bytes 1572868
  147.0 79.4 %all-reduce.12.cloned.1.call-start = ((), (), s32[]{:S(2)}) async-start(), calls=%async_computation.7 | async-start | bytes 524288 | tf_op jit(solution)/shard_map/psum | solution.py:114
  182.4 8.4 %collective-permute-start = (bf16[256,512]{1,0:T(8,128)(2,1)S(1)}, bf16[256,512]{1,0:T(8,128)(2,1)S(1)}, u32[]{:S(2)}, u32[]{:S(2)}) collective-permute-start(bf16[256,512]{1,0:T(8,128)(2,1)S(1)} %get-tuple-element.13), channel_id=1, source_target_pairs={{16,0},{17,1},{18,2},{19,3},{20,4},{21,5},{22,6},{23,7},{24,8},{25... | collective-permute-start | bytes 786440 | tf_op jit(solution)/shard_map/ppermute | solution.py:12
  191.8 34.6 %copy-start.17 = (bf16[256,512]{1,0:T(8,128)(2,1)}, bf16[256,512]{1,0:T(8,128)(2,1)S(1)}, u32[]{:S(2)}) copy-start(bf16[256,512]{1,0:T(8,128)(2,1)S(1)} %slice_select_fusion.1) | copy-start | bytes 786436
  194.0 79.5 %all-reduce.14.cloned.1.call-start = ((), (), s32[]{:S(2)}) async-start(), calls=%async_computation.8 | async-start | bytes 524288 | tf_op jit(solution)/shard_map/psum | solution.py:114
  228.3 8.5 %collective-permute-start.1 = (bf16[256,512]{1,0:T(8,128)(2,1)S(1)}, bf16[256,512]{1,0:T(8,128)(2,1)}, u32[]{:S(2)}, u32[]{:S(2)}) collective-permute-start(bf16[256,512]{1,0:T(8,128)(2,1)S(1)} %get-tuple-element.11), channel_id=1, source_target_pairs={{16,0},{17,1},{18,2},{19,3},{20,4},{21,5},{22,6},{23,7},{24,8},{25... | collective-permute-start | bytes 786440 | tf_op jit(solution)/shard_map/ppermute | solution.py:12
  241.0 79.5 %all-reduce.16.cloned.1.call-start = ((), (), s32[]{:S(2)}) async-start(), calls=%async_computation.9 | async-start | bytes 524288 | tf_op jit(solution)/shard_map/psum | solution.py:114
  275.4 8.7 %collective-permute-start.2 = (bf16[256,512]{1,0:T(8,128)(2,1)}, bf16[256,512]{1,0:T(8,128)(2,1)}, u32[]{:S(2)}, u32[]{:S(2)}) collective-permute-start(bf16[256,512]{1,0:T(8,128)(2,1)} %get-tuple-element.9), channel_id=1, source_target_pairs={{16,0},{17,1},{18,2},{19,3},{20,4},{21,5},{22,6},{23,7},{24,8},{25... | collective-permute-start | bytes 786440 | tf_op jit(solution)/shard_map/ppermute | solution.py:12
  276.7 9.2 %copy-start.31 = (bf16[1,512,512]{2,1,0:T(8,128)(2,1)S(1)}, bf16[1,512,512]{2,1,0:T(8,128)(2,1)}, u32[]{:S(2)}) copy-start(bf16[1,512,512]{2,1,0:T(8,128)(2,1)} %param.11) | copy-start | bytes 1572868
  277.0 9.3 %copy-start.25 = (f32[256,512]{1,0:T(8,128)}, f32[256,512]{1,0:T(8,128)S(1)}, u32[]{:S(2)}) copy-start(f32[256,512]{1,0:T(8,128)S(1)} %fusion.26) | copy-start | bytes 1572868
  288.1 79.5 %all-reduce.18.cloned.1.call-start = ((), (), s32[]{:S(2)}) async-start(), calls=%async_computation.10 | async-start | bytes 524288 | tf_op jit(solution)/shard_map/psum | solution.py:114
  322.5 8.7 %collective-permute-start.3 = (bf16[256,512]{1,0:T(8,128)(2,1)}, bf16[256,512]{1,0:T(8,128)(2,1)}, u32[]{:S(2)}, u32[]{:S(2)}) collective-permute-start(bf16[256,512]{1,0:T(8,128)(2,1)} %get-tuple-element.7), channel_id=1, source_target_pairs={{16,0},{17,1},{18,2},{19,3},{20,4},{21,5},{22,6},{23,7},{24,8},{25... | collective-permute-start | bytes 786440 | tf_op jit(solution)/shard_map/ppermute | solution.py:12
  324.0 9.0 %copy-start.32 = (bf16[1,512,512]{2,1,0:T(8,128)(2,1)S(1)}, bf16[1,512,512]{2,1,0:T(8,128)(2,1)}, u32[]{:S(2)}) copy-start(bf16[1,512,512]{2,1,0:T(8,128)(2,1)} %param.11) | copy-start | bytes 1572868
  324.3 9.1 %copy-start.26 = (f32[256,512]{1,0:T(8,128)}, f32[256,512]{1,0:T(8,128)S(1)}, u32[]{:S(2)}) copy-start(f32[256,512]{1,0:T(8,128)S(1)} %fusion.23) | copy-start | bytes 1572868
  335.2 62.0 %reduce-scatter.4.cloned.1.call-start = ((), (), s32[]{:S(2)}) async-start(), calls=%async_computation.4 | async-start | bytes 1310720 | tf_op jit(solution)/shard_map/reduce_scatter | solution.py:82
  339.2 81.2 %reduce-scatter.6.cloned.1.call-start = ((), (), s32[]{:S(2)}) async-start(), calls=%async_computation.12 | async-start | bytes 655360 | tf_op jit(solution)/shard_map/reduce_scatter | solution.py:128
  345.3 97.4 %reduce-scatter.8.cloned.1.call-start = ((), (), s32[]{:S(2)}) async-start(), calls=%async_computation.13 | async-start | bytes 655360 | tf_op jit(solution)/shard_map/reduce_scatter | solution.py:131
  350.5 132.9 %all-reduce.20.cloned.1.call-start = ((), (), s32[]{:S(2)}) async-start(), calls=%async_computation.11 | async-start | bytes 2097152 | tf_op jit(solution)/shard_map/psum | solution.py:17
  367.6 29.6 %copy-start.5 = (bf16[256,512]{1,0:T(8,128)(2,1)S(1)}, bf16[256,512]{1,0:T(8,128)(2,1)}, u32[]{:S(2)}) copy-start(bf16[256,512]{1,0:T(8,128)(2,1)} %param.7) | copy-start | bytes 786436
  (24 other events, 50.3 us)
Sparse Core Ops, SparseCore 0:
  10.4 30.6 all-gather.1
  90.8 50.3 all-reduce.7
  147.2 32.3 all-reduce.9
  194.1 32.2 all-reduce.11
  241.1 32.2 all-reduce.13
  288.2 32.2 all-reduce.15
  335.3 32.2 all-reduce.17
  369.9 27.2 reduce-scatter.3
  400.1 20.3 reduce-scatter.5
  422.5 20.0 reduce-scatter.7
  445.0 38.3 all-reduce.19
where the time goes:
time: 493 us; the launch traced here: 492 us
  waiting for transfers between devices  358 us (73%)
  other arithmetic  39.4 us (8%)
  blocking collectives  31 us (6%)
  matrix products  30.8 us (6%)
  between operations  15.1 us (3%)
  local copies, waits for them, and re-layouts  12.1 us (2%)
  starting transfers between devices  5.75 us (1%)
    psum x5, waiting for transfers between devices, body(): summed = lax.psum(unit_share.astype(jnp.bfloat16), 'mp').astype(jnp.float32)  147 us
    psum x1, waiting for transfers between devices, body(): text_unit_grad = lax.psum(text_share, 'mp')  49.2 us
    psum x1, waiting for transfers between devices, spread(): return lax.psum(kept, axis)  39.1 us
    all_gather x1, waiting for transfers between devices, body(): columns = lax.all_gather(image_low, 'dp', axis=0, tiled=True)  28.6 us
    ppermute x4, waiting for transfers between devices, shifted(): return lax.ppermute(block, axis, route)  27.7 us
    reduce_scatter x1, waiting for transfers between devices, body(): lax.psum_scatter((logit_mult * contract_rows(score_grad, text_low)).astyp...  25.4 us
    reduce_scatter x1, waiting for transfers between devices, body(): lax.psum_scatter(grad_second.astype(jnp.bfloat16), 'dp', scatter_dimensio...  20.6 us
    reduce_scatter x1, waiting for transfers between devices, body(): lax.psum_scatter(grad_first.astype(jnp.bfloat16), 'dp', scatter_dimension...  20.2 us
  transfers between devices with their start and end apart: 15, of which 15 were waited for; matrix products, arithmetic and copies ran while one was open for 6% of the time, Pallas kernels for 0%

commit v1 on v0

--- a/solution.py
+++ b/solution.py
@@ -111,7 +111,9 @@
         back_grad = contract_cols(grad_now, w_second)
         pre_grad = (back_grad * quick_slope(pre_act)).astype(jnp.bfloat16)
         unit_share = contract_cols(pre_grad, w_first)
-        summed = lax.psum(unit_share.astype(jnp.bfloat16), "mp").astype(jnp.float32)
+        summed = jnp.sum(lax.all_gather(unit_share.astype(jnp.bfloat16), "mp"), axis=0).astype(
+            jnp.float32
+        )
         grad_prev = (grad_now.astype(jnp.float32) + summed).astype(jnp.bfloat16)
         weight = active.astype(jnp.float32)
         grad_first = grad_first + weight * contract_rows(inputs_now, pre_grad)

time: 493 us -> 425 us (0.86)
  waiting for transfers between devices: 358 us -> 282 us
  other arithmetic: 39.4 us -> 47.9 us
    psum x5 -> x0, waiting for transfers between devices: 147 us -> none  [body(): summed = lax.psum(unit_share.astype(jnp.bfloat16), 'mp').astype(jnp.float32)]
    all_gather x0 -> x5, waiting for transfers between devices: none -> 64.9 us  [body(): lax.all_gather(unit_share.astype(jnp.bfloat16), 'mp')]
    reduce_sum x0 -> x5, other arithmetic: none -> 8.66 us  [body(): jnp.sum(lax.all_gather(unit_share.astype(jnp.bfloat16), 'mp'), axis=0)]
    ppermute x4, waiting for transfers between devices: 27.7 us -> 35.6 us  [shifted(): return lax.ppermute(block, axis, route)]
  transfers between devices with their start and end apart: 15 -> 15, of which waited for: 15 -> 15; matrix products, arithmetic and copies ran while one was open for 6% -> 7% of each run, Pallas kernels for 0% -> 0%
where the time goes in v1:
time: 425 us; the launch traced here: 424 us
  waiting for transfers between devices  282 us (66%)
  other arithmetic  47.9 us (11%)
  blocking collectives  31 us (7%)
  matrix products  29.8 us (7%)
  between operations  15.2 us (4%)
  local copies, waits for them, and re-layouts  12.1 us (3%)
  starting transfers between devices  5.75 us (1%)
    all_gather x5, waiting for transfers between devices, body(): lax.all_gather(unit_share.astype(jnp.bfloat16), 'mp')  64.9 us
    psum x1, waiting for transfers between devices, body(): text_unit_grad = lax.psum(text_share, 'mp')  49.2 us
    psum x1, waiting for transfers between devices, spread(): return lax.psum(kept, axis)  39.1 us
    ppermute x4, waiting for transfers between devices, shifted(): return lax.ppermute(block, axis, route)  35.6 us
    all_gather x1, waiting for transfers between devices, body(): columns = lax.all_gather(image_low, 'dp', axis=0, tiled=True)  28.6 us
    reduce_scatter x1, waiting for transfers between devices, body(): lax.psum_scatter((logit_mult * contract_rows(score_grad, text_low)).astyp...  24 us
    reduce_scatter x1, waiting for transfers between devices, body(): lax.psum_scatter(grad_second.astype(jnp.bfloat16), 'dp', scatter_dimensio...  20.6 us
    reduce_scatter x1, waiting for transfers between devices, body(): lax.psum_scatter(grad_first.astype(jnp.bfloat16), 'dp', scatter_dimension...  20.2 us
  transfers between devices with their start and end apart: 15, of which 15 were waited for; matrix products, arithmetic and copies ran while one was open for 7% of the time, Pallas kernels for 0%

profile of v1, /device:TPU:0, one launch (start us, length us, event | category | flops | bytes accessed | tf_op | source)
XLA Modules:
  0.0 424.1 jit_solution(6180086538516974225)
XLA Ops:
  12.5 28.6 %all-gather.12.cloned.1.call-done = bf16[1024,512]{1,0:T(8,128)(2,1)} async-done(((bf16[256,512]{1,0:T(8,128)(2,1)}), bf16[1024,512]{1,0:T(8,128)(2,1)}) %all-gather.12.cloned.1.call-update) | async-done | bytes 1048592 | tf_op jit(solution)/shard_map/all_gather | solution.py:64
  41.1 4.5 %multiply_reduce_fusion.1 = (f32[1024]{0:T(1024)S(1)}, f32[1024,1024]{1,0:T(8,128)}) fusion(f32[]{:T(128)} %bitcast.92, bf16[1024,512]{1,0:T(8,128)(2,1)} %all-gather.12.cloned.1.call-done, f32[1024]{0:T(1024)S(1)} %add_sqrt_fusion, bf16[1024,512]{1,0:T(8,128)(2,1)S(1)} %copy-done.2), kind=kOutput, calls=%fused_computation.6 | convolution fusion | flops 1077410816 | bytes 6299652 | tf_op jit(solution)/shard_map/dot_general | solution.py:46
  45.7 6.0 %pmax.14 = f32[1024]{0:T(1024)S(1)} all-reduce(f32[1024]{0:T(1024)S(1)} %get-tuple-element.14), channel_id=1, replica_groups=mesh['section'=2,'dp'=4,'mp'=4] {'mp'}, use_global_device_ids=true, to_apply=%region_3.4 | all-reduce | flops 1024 | bytes 8192 | tf_op jit(solution)/shard_map/pmax | solution.py:71
  51.7 3.2 fusion
  54.9 10.9 %pmax.15 = f32[1024]{0:T(1024)S(1)} all-reduce(f32[1024]{0:T(1024)S(1)} %get-tuple-element.5), channel_id=1, replica_groups=mesh['section'=2,'dp'=4,'mp'=4] {'dp'}, use_global_device_ids=true, to_apply=%region_7.8 | all-reduce | flops 1024 | bytes 8192 | tf_op jit(solution)/shard_map/pmax | solution.py:72
  65.8 2.9 fusion.1
  68.7 8.4 %psum.29 = f32[1024]{0:T(1024)S(1)} all-reduce(f32[1024]{0:T(1024)S(1)} %fusion.1), channel_id=1, replica_groups=mesh['section'=2,'dp'=4,'mp'=4] {'dp'}, use_global_device_ids=true, to_apply=%region_9.10 | all-reduce | flops 1024 | bytes 8192 | tf_op jit(solution)/shard_map/psum | solution.py:75
  77.1 5.7 %psum.28 = f32[1024]{0:T(1024)S(1)} all-reduce(f32[1024]{0:T(1024)S(1)} %get-tuple-element.4), channel_id=1, replica_groups=mesh['section'=2,'dp'=4,'mp'=4] {'mp'}, use_global_device_ids=true, to_apply=%region_5.6 | all-reduce | flops 1024 | bytes 8192 | tf_op jit(solution)/shard_map/psum | solution.py:73
  82.7 3.9 subtract_convert_fusion
  88.0 2.6 convolution_multiply_fusion
  92.0 49.2 %all-reduce.3.cloned.1.call-done = f32[1024,512]{1,0:T(8,128)} async-done(((f32[1024,512]{1,0:T(8,128)}), f32[1024,512]{1,0:T(8,128)}) %all-reduce.3.cloned.1.call-update) | async-done | bytes 2097168 | tf_op jit(solution)/shard_map/psum | solution.py:80
  147.1 16.9 %all-gather.14.cloned.1.call-done = bf16[1024,512]{1,0:T(8,128)(2,1)} async-done(((bf16[256,512]{1,0:T(8,128)(2,1)}), bf16[1024,512]{1,0:T(8,128)(2,1)}) %all-gather.14.cloned.1.call-update) | async-done | bytes 1048592 | tf_op jit(solution)/shard_map/all_gather | solution.py:114
  169.8 8.7 %collective-permute-done = bf16[256,512]{1,0:T(8,128)(2,1)S(1)} collective-permute-done((bf16[256,512]{1,0:T(8,128)(2,1)S(1)}, bf16[256,512]{1,0:T(8,128)(2,1)S(1)}, u32[]{:S(2)}, u32[]{:S(2)}) %collective-permute-start) | collective-permute-done | bytes 262176 | tf_op jit(solution)/shard_map/ppermute | solution.py:12
  181.8 15.9 %all-gather.16.cloned.1.call-done = bf16[1024,512]{1,0:T(8,128)(2,1)} async-done(((bf16[256,512]{1,0:T(8,128)(2,1)}), bf16[1024,512]{1,0:T(8,128)(2,1)}) %all-gather.16.cloned.1.call-update) | async-done | bytes 1048592 | tf_op jit(solution)/shard_map/all_gather | solution.py:114
  202.5 8.8 %collective-permute-done.1 = bf16[256,512]{1,0:T(8,128)(2,1)} collective-permute-done((bf16[256,512]{1,0:T(8,128)(2,1)S(1)}, bf16[256,512]{1,0:T(8,128)(2,1)}, u32[]{:S(2)}, u32[]{:S(2)}) %collective-permute-start.1) | collective-permute-done | bytes 262176 | tf_op jit(solution)/shard_map/ppermute | solution.py:12
  214.6 15.9 %all-gather.18.cloned.1.call-done = bf16[1024,512]{1,0:T(8,128)(2,1)} async-done(((bf16[256,512]{1,0:T(8,128)(2,1)}), bf16[1024,512]{1,0:T(8,128)(2,1)}) %all-gather.18.cloned.1.call-update) | async-done | bytes 1048592 | tf_op jit(solution)/shard_map/all_gather | solution.py:114
  236.2 9.0 %collective-permute-done.2 = bf16[256,512]{1,0:T(8,128)(2,1)} collective-permute-done((bf16[256,512]{1,0:T(8,128)(2,1)}, bf16[256,512]{1,0:T(8,128)(2,1)}, u32[]{:S(2)}, u32[]{:S(2)}) %collective-permute-start.2) | collective-permute-done | bytes 262176 | tf_op jit(solution)/shard_map/ppermute | solution.py:12
  249.4 15.7 %all-gather.20.cloned.1.call-done = bf16[1024,512]{1,0:T(8,128)(2,1)} async-done(((bf16[256,512]{1,0:T(8,128)(2,1)}), bf16[1024,512]{1,0:T(8,128)(2,1)}) %all-gather.20.cloned.1.call-update) | async-done | bytes 1048592 | tf_op jit(solution)/shard_map/all_gather | solution.py:114
  270.9 9.0 %collective-permute-done.3 = bf16[256,512]{1,0:T(8,128)(2,1)} collective-permute-done((bf16[256,512]{1,0:T(8,128)(2,1)}, bf16[256,512]{1,0:T(8,128)(2,1)}, u32[]{:S(2)}, u32[]{:S(2)}) %collective-permute-start.3) | collective-permute-done | bytes 262176 | tf_op jit(solution)/shard_map/ppermute | solution.py:12
  283.9 4.0 multiply_convert_fusion
  305.4 24.0 %reduce-scatter.4.cloned.1.call-done = bf16[256,512]{1,0:T(8,128)(2,1)} async-done(((bf16[1024,512]{1,0:T(8,128)(2,1)}), bf16[256,512]{1,0:T(8,128)(2,1)}) %reduce-scatter.4.cloned.1.call-update) | async-done | bytes 262160 | tf_op jit(solution)/shard_map/reduce_scatter | solution.py:82
  332.5 20.2 %reduce-scatter.6.cloned.1.call-done = bf16[128,512]{1,0:T(8,128)(2,1)} async-done(((bf16[512,512]{1,0:T(8,128)(2,1)}), bf16[128,512]{1,0:T(8,128)(2,1)}) %reduce-scatter.6.cloned.1.call-update) | async-done | bytes 131088 | tf_op jit(solution)/shard_map/reduce_scatter | solution.py:130
  354.3 20.6 %reduce-scatter.8.cloned.1.call-done = bf16[128,512]{1,0:T(8,128)(2,1)} async-done(((bf16[512,512]{1,0:T(8,128)(2,1)}), bf16[128,512]{1,0:T(8,128)(2,1)}) %reduce-scatter.8.cloned.1.call-update) | async-done | bytes 131088 | tf_op jit(solution)/shard_map/reduce_scatter | solution.py:133
  376.6 39.1 %all-reduce.5.cloned.1.call-done = bf16[1024,512]{1,0:T(8,128)(2,1)} async-done(((bf16[1024,512]{1,0:T(8,128)(2,1)}), bf16[1024,512]{1,0:T(8,128)(2,1)}) %all-reduce.5.cloned.1.call-update) | async-done | bytes 1048592 | tf_op jit(solution)/shard_map/psum | solution.py:17
  (149 shorter events, 75.1 us)
Async XLA Ops:
  7.2 83.5 %copy-start = (bf16[1,1024,512]{2,1,0:T(8,128)(2,1)S(1)}, bf16[1,1024,512]{2,1,0:T(8,128)(2,1)}, u32[]{:S(2)}) copy-start(bf16[1,1024,512]{2,1,0:T(8,128)(2,1)} %param.9) | copy-start | bytes 3145732
  7.2 34.0 %copy-start.2 = (bf16[1024,512]{1,0:T(8,128)(2,1)S(1)}, bf16[1024,512]{1,0:T(8,128)(2,1)}, u32[]{:S(2)}) copy-start(bf16[1024,512]{1,0:T(8,128)(2,1)} %param.6) | copy-start | bytes 3145732
  7.2 33.9 %all-gather.12.cloned.1.call-start = ((), (), s32[]{:S(2)}) async-start(), calls=%async_computation.3 | async-start | bytes 1310720 | tf_op jit(solution)/shard_map/all_gather | solution.py:64
  10.3 130.9 %all-reduce.3.cloned.1.call-start = ((), (), s32[]{:S(2)}) async-start(), calls=%async_computation.5 | async-start | bytes 4194304 | tf_op jit(solution)/shard_map/psum | solution.py:80
  90.6 73.3 %all-gather.14.cloned.1.call-start = ((), (), s32[]{:S(2)}) async-start(), calls=%async_computation.9 | async-start | bytes 1310720 | tf_op jit(solution)/shard_map/all_gather | solution.py:114
  91.9 51.9 %copy-start.23 = (f32[256,512]{1,0:T(8,128)}, f32[256,512]{1,0:T(8,128)S(1)}, u32[]{:S(2)}) copy-start(f32[256,512]{1,0:T(8,128)S(1)} %fusion.35) | copy-start | bytes 1572868
  147.0 50.6 %all-gather.16.cloned.1.call-start = ((), (), s32[]{:S(2)}) async-start(), calls=%async_computation.10 | async-start | bytes 1310720 | tf_op jit(solution)/shard_map/all_gather | solution.py:114
  168.2 10.3 %collective-permute-start = (bf16[256,512]{1,0:T(8,128)(2,1)S(1)}, bf16[256,512]{1,0:T(8,128)(2,1)S(1)}, u32[]{:S(2)}, u32[]{:S(2)}) collective-permute-start(bf16[256,512]{1,0:T(8,128)(2,1)S(1)} %get-tuple-element.13), channel_id=1, source_target_pairs={{16,0},{17,1},{18,2},{19,3},{20,4},{21,5},{22,6},{23,7},{24,8},{25... | collective-permute-start | bytes 786440 | tf_op jit(solution)/shard_map/ppermute | solution.py:12
  179.5 19.6 %copy-start.17 = (bf16[256,512]{1,0:T(8,128)(2,1)}, bf16[256,512]{1,0:T(8,128)(2,1)S(1)}, u32[]{:S(2)}) copy-start(bf16[256,512]{1,0:T(8,128)(2,1)S(1)} %slice_select_fusion.1) | copy-start | bytes 786436
  181.7 48.8 %all-gather.18.cloned.1.call-start = ((), (), s32[]{:S(2)}) async-start(), calls=%async_computation.11 | async-start | bytes 1310720 | tf_op jit(solution)/shard_map/all_gather | solution.py:114
  200.9 10.4 %collective-permute-start.1 = (bf16[256,512]{1,0:T(8,128)(2,1)S(1)}, bf16[256,512]{1,0:T(8,128)(2,1)}, u32[]{:S(2)}, u32[]{:S(2)}) collective-permute-start(bf16[256,512]{1,0:T(8,128)(2,1)S(1)} %get-tuple-element.11), channel_id=1, source_target_pairs={{16,0},{17,1},{18,2},{19,3},{20,4},{21,5},{22,6},{23,7},{24,8},{25... | collective-permute-start | bytes 786440 | tf_op jit(solution)/shard_map/ppermute | solution.py:12
  214.6 50.6 %all-gather.20.cloned.1.call-start = ((), (), s32[]{:S(2)}) async-start(), calls=%async_computation.12 | async-start | bytes 1310720 | tf_op jit(solution)/shard_map/all_gather | solution.py:114
  234.6 10.6 %collective-permute-start.2 = (bf16[256,512]{1,0:T(8,128)(2,1)}, bf16[256,512]{1,0:T(8,128)(2,1)}, u32[]{:S(2)}, u32[]{:S(2)}) collective-permute-start(bf16[256,512]{1,0:T(8,128)(2,1)} %get-tuple-element.9), channel_id=1, source_target_pairs={{16,0},{17,1},{18,2},{19,3},{20,4},{21,5},{22,6},{23,7},{24,8},{25... | collective-permute-start | bytes 786440 | tf_op jit(solution)/shard_map/ppermute | solution.py:12
  235.9 11.1 %copy-start.32 = (bf16[1,512,512]{2,1,0:T(8,128)(2,1)S(1)}, bf16[1,512,512]{2,1,0:T(8,128)(2,1)}, u32[]{:S(2)}) copy-start(bf16[1,512,512]{2,1,0:T(8,128)(2,1)} %param.11) | copy-start | bytes 1572868
  236.2 11.2 %copy-start.25 = (f32[256,512]{1,0:T(8,128)}, f32[256,512]{1,0:T(8,128)S(1)}, u32[]{:S(2)}) copy-start(f32[256,512]{1,0:T(8,128)S(1)} %fusion.26) | copy-start | bytes 1572868
  249.2 50.6 %all-gather.22.cloned.1.call-start = ((), (), s32[]{:S(2)}) async-start(), calls=%async_computation.13 | async-start | bytes 1310720 | tf_op jit(solution)/shard_map/all_gather | solution.py:114
  269.3 10.6 %collective-permute-start.3 = (bf16[256,512]{1,0:T(8,128)(2,1)}, bf16[256,512]{1,0:T(8,128)(2,1)}, u32[]{:S(2)}, u32[]{:S(2)}) collective-permute-start(bf16[256,512]{1,0:T(8,128)(2,1)} %get-tuple-element.7), channel_id=1, source_target_pairs={{16,0},{17,1},{18,2},{19,3},{20,4},{21,5},{22,6},{23,7},{24,8},{25... | collective-permute-start | bytes 786440 | tf_op jit(solution)/shard_map/ppermute | solution.py:12
  270.6 11.1 %copy-start.33 = (bf16[1,512,512]{2,1,0:T(8,128)(2,1)S(1)}, bf16[1,512,512]{2,1,0:T(8,128)(2,1)}, u32[]{:S(2)}) copy-start(bf16[1,512,512]{2,1,0:T(8,128)(2,1)} %param.11) | copy-start | bytes 1572868
  270.9 11.2 %copy-start.26 = (f32[256,512]{1,0:T(8,128)}, f32[256,512]{1,0:T(8,128)S(1)}, u32[]{:S(2)}) copy-start(f32[256,512]{1,0:T(8,128)S(1)} %fusion.23) | copy-start | bytes 1572868
  283.9 45.6 %reduce-scatter.4.cloned.1.call-start = ((), (), s32[]{:S(2)}) async-start(), calls=%async_computation.4 | async-start | bytes 1310720 | tf_op jit(solution)/shard_map/reduce_scatter | solution.py:82
  288.0 64.7 %reduce-scatter.6.cloned.1.call-start = ((), (), s32[]{:S(2)}) async-start(), calls=%async_computation.7 | async-start | bytes 655360 | tf_op jit(solution)/shard_map/reduce_scatter | solution.py:130
  294.0 80.9 %reduce-scatter.8.cloned.1.call-start = ((), (), s32[]{:S(2)}) async-start(), calls=%async_computation.8 | async-start | bytes 655360 | tf_op jit(solution)/shard_map/reduce_scatter | solution.py:133
  299.2 116.4 %all-reduce.5.cloned.1.call-start = ((), (), s32[]{:S(2)}) async-start(), calls=%async_computation.6 | async-start | bytes 2097152 | tf_op jit(solution)/shard_map/psum | solution.py:17
  301.3 28.2 %copy-start.5 = (bf16[256,512]{1,0:T(8,128)(2,1)S(1)}, bf16[256,512]{1,0:T(8,128)(2,1)}, u32[]{:S(2)}) copy-start(bf16[256,512]{1,0:T(8,128)(2,1)} %param.7) | copy-start | bytes 786436
  (25 other events, 64.4 us)
Sparse Core Ops, SparseCore 0:
  10.4 30.6 all-gather.11
  90.8 50.3 all-reduce.2
  147.2 16.7 all-gather.13
  181.8 15.7 all-gather.15
  214.7 15.7 all-gather.17
  249.3 15.7 all-gather.19
  284.0 15.7 all-gather.21
  302.1 27.2 reduce-scatter.3
  332.3 20.3 reduce-scatter.5
  354.8 20.1 reduce-scatter.7
  377.2 38.3 all-reduce.4
